TPU v7x, 32 devices: a whole 2x2x4 slice. The times are simulated.
32 devices in a mesh: groups: 2 (over x), seq: 16 (over z, y, core).
Axes of the slice: x: 2, y: 2, z: 4, core: 2. Of those that a mesh axis runs over, the one named last changes fastest.
Arguments:
- video_qkv: bfloat16 [8, 16, 3, 3072, 128], P('groups', None, None, 'seq'), parts along dimension 0, may hold values from -9 to 9
- video_cross: bfloat16 [8, 16, 3, 3072, 128], P('groups', None, None, 'seq'), parts along dimension 0, may hold values from -9 to 9
- audio_qkv: bfloat16 [8, 16, 3, 768, 128], P('groups', None, None, 'seq'), parts along dimension 0, may hold values from -9 to 9
- audio_cross: bfloat16 [8, 16, 3, 768, 128], P('groups', None, None, 'seq'), parts along dimension 0, may hold values from -9 to 9
- lengths: int32 [2, 8], P(None, 'groups'), parts along dimension 1, may hold values from 384 to 3072, as said below
- timestep: int32 [2], P('groups'), parts along dimension 0, may hold values from 0 to 49
- gate_table: float32 [50, 4, 16, 128], replicated, may hold values from -4 to 4
Outputs:
- video_out: bfloat16 [8, 16, 3072, 128], P('groups', None, 'seq'), parts along dimension 0
- audio_out: bfloat16 [8, 16, 768, 128], P('groups', None, 'seq'), parts along dimension 0
There are 2 independent parts, one for each index of `groups`. A program takes and returns all parts, laid end to end along the dimension named above; an argument that names none is the same for every part. Nothing has to cross between parts.
Inputs may be any that keep to these rules, and one draw needn't show every extreme that they name: `lengths`: row 0 holds each clip's valid video token count, row 1 its valid audio token count; every count is at least half of its tower's length (3072 or 768), and in every draw some clip has all 3072 video tokens and some clip all 768 audio tokens valid.
All inputs are finite; a program needn't handle non-finite values.
Results may differ from a plain program's by a relative error of at most 0.0085.
Values may be sent and summed in bfloat16 or wider, within the bound.
A program may use at most 128 MiB of HBM per device.

v0:
```python
import math

import jax
import jax.numpy as jnp
from jax import lax
from jax.sharding import PartitionSpec as P


def attend(queries, key_rows, values, keep_len):
    row_count = queries.shape[0]
    block_rows = row_count if row_count <= 1024 else math.gcd(row_count, 1024)
    score_scale = 1.0 / math.sqrt(queries.shape[1])
    columns = jnp.arange(key_rows.shape[0], dtype=jnp.int32)
    visible = columns[None, :] < keep_len
    blocks = queries.reshape(row_count // block_rows, block_rows, queries.shape[1])

    def one_block(query_block):
        scores = (
            lax.dot_general(
                query_block, key_rows, (((1,), (1,)), ((), ())), preferred_element_type=jnp.float32
            )
            * score_scale
        )
        scores = jnp.where(visible, scores, -1e30)
        row_max = jnp.max(scores, axis=1, keepdims=True)
        weights = jnp.exp(scores - row_max)
        row_total = jnp.sum(weights, axis=1, keepdims=True)
        shares = (weights / row_total).astype(jnp.bfloat16)
        return jnp.dot(shares, values, preferred_element_type=jnp.float32).astype(jnp.bfloat16)

    return lax.map(one_block, blocks).reshape(row_count, queries.shape[1])


def pair_outputs(bundle):
    video_set, video_far, audio_set, audio_far, video_len, audio_len = bundle
    self_video = attend(video_set[0], video_set[1], video_set[2], video_len)
    cross_video = attend(video_far[0], audio_far[1], audio_far[2], audio_len)
    self_audio = attend(audio_set[0], audio_set[1], audio_set[2], audio_len)
    cross_audio = attend(audio_far[0], video_far[1], video_far[2], video_len)
    return (self_video, cross_video, self_audio, cross_audio)


def mix_pairs(self_part, cross_part, gate_self, gate_cross):
    mixed_sum = gate_self[:, None, :] * self_part.astype(jnp.float32) + gate_cross[
        :, None, :
    ] * cross_part.astype(jnp.float32)
    return mixed_sum.astype(jnp.bfloat16)


def on_device(video_qkv, video_cross, audio_qkv, audio_cross, lengths, timestep, gate_table):
    group_size = lax.axis_size("seq")
    clip_count, head_count = (video_qkv.shape[0], video_qkv.shape[1])
    video_rows, audio_rows, head_size = (video_qkv.shape[3], audio_qkv.shape[3], video_qkv.shape[4])
    pair_count = clip_count * head_count
    pair_local = pair_count // group_size

    def to_pairs(tensor):
        return tensor.reshape((pair_count,) + tensor.shape[2:])

    video_set, video_far = (
        lax.all_to_all(to_pairs(video_qkv), "seq", split_axis=0, concat_axis=2, tiled=True),
        lax.all_to_all(to_pairs(video_cross), "seq", split_axis=0, concat_axis=2, tiled=True),
    )
    audio_set, audio_far = (
        lax.all_to_all(to_pairs(audio_qkv), "seq", split_axis=0, concat_axis=2, tiled=True),
        lax.all_to_all(to_pairs(audio_cross), "seq", split_axis=0, concat_axis=2, tiled=True),
    )
    pair_ids = lax.axis_index("seq") * pair_local + jnp.arange(pair_local, dtype=jnp.int32)
    clip_hot = (pair_ids // head_count)[:, None] == jnp.arange(clip_count, dtype=jnp.int32)[None, :]
    video_lens = jnp.sum(jnp.where(clip_hot, lengths[0][None, :], 0), axis=1)
    audio_lens = jnp.sum(jnp.where(clip_hot, lengths[1][None, :], 0), axis=1)
    self_video, cross_video, self_audio, cross_audio = lax.map(
        pair_outputs, (video_set, video_far, audio_set, audio_far, video_lens, audio_lens)
    )
    step_ids = jnp.arange(gate_table.shape[0], dtype=jnp.int32)
    gate_rows = jnp.sum(
        jnp.where((step_ids == timestep[0])[:, None, None, None], gate_table, 0.0), axis=0
    )
    head_hot = (pair_ids % head_count)[:, None] == jnp.arange(head_count, dtype=jnp.int32)[None, :]
    pair_gates = jnp.sum(
        jnp.where(head_hot[None, :, :, None], gate_rows[:, None, :, :], 0.0), axis=2
    )
    mix_video = mix_pairs(self_video, cross_video, pair_gates[0], pair_gates[1])
    mix_audio = mix_pairs(self_audio, cross_audio, pair_gates[2], pair_gates[3])
    video_out = lax.all_to_all(mix_video, "seq", split_axis=1, concat_axis=0, tiled=True).reshape(
        clip_count, head_count, video_rows, head_size
    )
    audio_out = lax.all_to_all(mix_audio, "seq", split_axis=1, concat_axis=0, tiled=True).reshape(
        clip_count, head_count, audio_rows, head_size
    )
    return (video_out, audio_out)


def solution(mesh):
    in_specs = (
        P("groups", None, None, "seq", None),
        P("groups", None, None, "seq", None),
        P("groups", None, None, "seq", None),
        P("groups", None, None, "seq", None),
        P(None, "groups"),
        P("groups"),
        P(),
    )
    out_specs = (P("groups", None, "seq", None), P("groups", None, "seq", None))
    return jax.shard_map(
        on_device, mesh=mesh, in_specs=in_specs, out_specs=out_specs, check_vma=False
    )
```

profile of v0, /device:TPU:13, one launch (start us, length us, event | category | flops | bytes accessed | tf_op | source)
XLA Modules:
  0.0 936.6 jit_solution(4870514714091157007)
XLA Ops:
  0.6 59.8 %all_to_all.102 = bf16[64,3,48,128]{3,2,1,0:T(8,128)(2,1)} all-to-all(bf16[64,3,48,128]{3,2,1,0:T(8,128)(2,1)} %bitcast.178), channel_id=1, replica_groups=mesh['groups'=2,'seq'=16] {'seq'}, dimensions={0} | all-to-all | bytes 4718592 | tf_op jit(solution)/shard_map/all_to_all | solution.py:66
  60.4 57.9 %all_to_all.103 = bf16[64,3,48,128]{3,2,1,0:T(8,128)(2,1)S(1)} all-to-all(bf16[64,3,48,128]{3,2,1,0:T(8,128)(2,1)} %bitcast.179), channel_id=1, replica_groups=mesh['groups'=2,'seq'=16] {'seq'}, dimensions={0} | all-to-all | bytes 4718592 | tf_op jit(solution)/shard_map/all_to_all | solution.py:65
  118.3 209.5 %all_to_all.104 = bf16[64,3,192,128]{3,2,1,0:T(8,128)(2,1)} all-to-all(bf16[64,3,192,128]{3,2,1,0:T(8,128)(2,1)S(1)} %bitcast.172), channel_id=1, replica_groups=mesh['groups'=2,'seq'=16] {'seq'}, dimensions={0} | all-to-all | bytes 18874368 | tf_op jit(solution)/shard_map/all_to_all | solution.py:61
  327.8 5.8 all-to-all-start.1
  337.6 3.6 copy.41
  343.1 10.2 %copy.39 = bf16[4,3,16,192,128]{4,3,2,1,0:T(8,128)(2,1)} copy(bf16[4,3,16,192,128]{4,3,1,0,2:T(8,128)(2,1)} %bitcast.169) | data formatting | bytes 18874368 | tf_op jit(solution)/shard_map/all_to_all | solution.py:61
  353.3 185.2 %all-to-all-done.1 = bf16[64,3,192,128]{3,2,1,0:T(8,128)(2,1)} async-done(((bf16[64,3,192,128]{3,2,1,0:T(8,128)(2,1)}), bf16[64,3,192,128]{3,2,1,0:T(8,128)(2,1)}, u32[]{:S(2)}, u32[]{:S(2)}) %all-to-all-start.1) | async-done | bytes 9437216 | tf_op jit(solution)/shard_map/all_to_all | solution.py:62
  538.5 10.3 %copy.40 = bf16[4,3,16,192,128]{4,3,2,1,0:T(8,128)(2,1)} copy(bf16[4,3,16,192,128]{4,3,1,0,2:T(8,128)(2,1)} %bitcast.27) | data formatting | bytes 18874368 | tf_op jit(solution)/shard_map/all_to_all | solution.py:62
  548.8 280.8 %while.48 = (s32[]{:T(128)}, bf16[4,3072,128]{2,1,0:T(8,128)(2,1)}, bf16[4,3072,128]{2,1,0:T(8,128)(2,1)}, bf16[4,768,128]{2,1,0:T(8,128)(2,1)}, bf16[4,768,128]...) while((s32[]{:T(128)}, bf16[4,3072,128]{2,1,0:T(8,128)(2,1)}, ...), condition=%wide.region_17.18_spmd, body=%wide.region_4.17_spmd.sunk | while | flops 3606249984 | bytes 141142128 | solution.py:72
  550.7 2.9 fusion.73
  553.6 3.7 copy-done
  559.4 6.9 fusion.75
  572.9 3.0 dynamic-slice_bitcast_fusion.22
  577.0 9.9 %while.50 = (s32[]{:T(128)}, bf16[3,1024,128]{2,1,0:T(8,128)(2,1)S(1)}, bf16[3,1024,128]{2,1,0:T(8,128)(2,1)S(1)}, bf16[768,128]{1,0:T(8,128)(2,1)S(1)}, bf16[768,128]{1,0:T(8,128)(2,1)S(1)}, /*index=5*/s32[]{:T(128)}, s32[]{:T(128)}) while((s32[]{:T(128)}, bf16[3,1024,128]{2,1,0:T(8,128)(2,1)S(1)}, ...), condition=%wide.region_12.12_spmd.clone, body=%wide.region_9.11_spmd.clone.sunk | while | flops 412220160 | bytes 10378841 | solution.py:31
  588.0 30.1 %while.49 = (s32[]{:T(128)}, bf16[3,1024,128]{2,1,0:T(8,128)(2,1)S(1)}, bf16[3,1024,128]{2,1,0:T(8,128)(2,1)S(1)}, bf16[3072,128]{1,0:T(8,128)(2,1)S(1)}, bf16[3072,128]{1,0:T(8,128)(2,1)}, /*index=5*/s32[]{:T(128)}, s32[]{:T(128)}) while((s32[]{:T(128)}, bf16[3,1024,128]{2,1,0:T(8,128)(2,1)S(1)}, ...), condition=%wide.region_8.8_spmd.clone, body=%wide.region_5.7_spmd.clone.sunk | while | flops 1648493568 | bytes 43024500 | solution.py:31
  590.8 2.7 fusion.79
  593.6 4.4 fusion.80
  600.9 2.7 fusion.79
  603.6 4.4 fusion.80
  610.9 2.7 fusion.79
  613.6 4.4 fusion.80
  620.9 2.9 fusion.73
  623.8 3.7 copy-done
  629.6 6.8 fusion.75
  643.0 3.0 dynamic-slice_bitcast_fusion.22
  647.2 9.9 %while.50 = (s32[]{:T(128)}, bf16[3,1024,128]{2,1,0:T(8,128)(2,1)S(1)}, bf16[3,1024,128]{2,1,0:T(8,128)(2,1)S(1)}, bf16[768,128]{1,0:T(8,128)(2,1)S(1)}, bf16[768,128]{1,0:T(8,128)(2,1)S(1)}, /*index=5*/s32[]{:T(128)}, s32[]{:T(128)}) while((s32[]{:T(128)}, bf16[3,1024,128]{2,1,0:T(8,128)(2,1)S(1)}, ...), condition=%wide.region_12.12_spmd.clone, body=%wide.region_9.11_spmd.clone.sunk | while | flops 412220160 | bytes 10378841 | solution.py:31
  658.1 30.1 %while.49 = (s32[]{:T(128)}, bf16[3,1024,128]{2,1,0:T(8,128)(2,1)S(1)}, bf16[3,1024,128]{2,1,0:T(8,128)(2,1)S(1)}, bf16[3072,128]{1,0:T(8,128)(2,1)S(1)}, bf16[3072,128]{1,0:T(8,128)(2,1)}, /*index=5*/s32[]{:T(128)}, s32[]{:T(128)}) while((s32[]{:T(128)}, bf16[3,1024,128]{2,1,0:T(8,128)(2,1)S(1)}, ...), condition=%wide.region_8.8_spmd.clone, body=%wide.region_5.7_spmd.clone.sunk | while | flops 1648493568 | bytes 43024500 | solution.py:31
  661.0 2.7 fusion.79
  663.7 4.4 fusion.80
  671.0 2.7 fusion.79
  673.7 4.4 fusion.80
  681.0 2.7 fusion.79
  683.8 4.4 fusion.80
  691.1 2.9 fusion.73
  694.0 3.7 copy-done
  699.8 7.0 fusion.75
  710.7 2.6 fusion.72
  713.3 3.0 dynamic-slice_bitcast_fusion.22
  717.4 9.9 %while.50 = (s32[]{:T(128)}, bf16[3,1024,128]{2,1,0:T(8,128)(2,1)S(1)}, bf16[3,1024,128]{2,1,0:T(8,128)(2,1)S(1)}, bf16[768,128]{1,0:T(8,128)(2,1)S(1)}, bf16[768,128]{1,0:T(8,128)(2,1)S(1)}, /*index=5*/s32[]{:T(128)}, s32[]{:T(128)}) while((s32[]{:T(128)}, bf16[3,1024,128]{2,1,0:T(8,128)(2,1)S(1)}, ...), condition=%wide.region_12.12_spmd.clone, body=%wide.region_9.11_spmd.clone.sunk | while | flops 412220160 | bytes 10378841 | solution.py:31
  728.5 30.1 %while.49 = (s32[]{:T(128)}, bf16[3,1024,128]{2,1,0:T(8,128)(2,1)S(1)}, bf16[3,1024,128]{2,1,0:T(8,128)(2,1)S(1)}, bf16[3072,128]{1,0:T(8,128)(2,1)S(1)}, bf16[3072,128]{1,0:T(8,128)(2,1)}, /*index=5*/s32[]{:T(128)}, s32[]{:T(128)}) while((s32[]{:T(128)}, bf16[3,1024,128]{2,1,0:T(8,128)(2,1)S(1)}, ...), condition=%wide.region_8.8_spmd.clone, body=%wide.region_5.7_spmd.clone.sunk | while | flops 1648493568 | bytes 43024500 | solution.py:31
  731.3 2.7 fusion.79
  734.0 4.4 fusion.80
  741.3 2.7 fusion.79
  744.1 4.4 fusion.80
  751.3 2.7 fusion.79
  754.1 4.4 fusion.80
  761.4 2.9 fusion.73
  764.3 3.7 copy-done
  770.1 6.8 fusion.75
  780.9 2.6 fusion.72
  783.5 3.0 dynamic-slice_bitcast_fusion.22
  787.6 9.9 %while.50 = (s32[]{:T(128)}, bf16[3,1024,128]{2,1,0:T(8,128)(2,1)S(1)}, bf16[3,1024,128]{2,1,0:T(8,128)(2,1)S(1)}, bf16[768,128]{1,0:T(8,128)(2,1)S(1)}, bf16[768,128]{1,0:T(8,128)(2,1)S(1)}, /*index=5*/s32[]{:T(128)}, s32[]{:T(128)}) while((s32[]{:T(128)}, bf16[3,1024,128]{2,1,0:T(8,128)(2,1)S(1)}, ...), condition=%wide.region_12.12_spmd.clone, body=%wide.region_9.11_spmd.clone.sunk | while | flops 412220160 | bytes 10378841 | solution.py:31
  798.6 30.1 %while.49 = (s32[]{:T(128)}, bf16[3,1024,128]{2,1,0:T(8,128)(2,1)S(1)}, bf16[3,1024,128]{2,1,0:T(8,128)(2,1)S(1)}, bf16[3072,128]{1,0:T(8,128)(2,1)S(1)}, bf16[3072,128]{1,0:T(8,128)(2,1)}, /*index=5*/s32[]{:T(128)}, s32[]{:T(128)}) while((s32[]{:T(128)}, bf16[3,1024,128]{2,1,0:T(8,128)(2,1)S(1)}, ...), condition=%wide.region_8.8_spmd.clone, body=%wide.region_5.7_spmd.clone.sunk | while | flops 1648493568 | bytes 43024500 | solution.py:31
  801.4 2.7 fusion.79
  804.2 4.4 fusion.80
  811.5 2.7 fusion.79
  814.2 4.4 fusion.80
  821.5 2.7 fusion.79
  824.2 4.4 fusion.80
  832.8 4.8 all-to-all-start.5
  837.6 4.1 add_convert_fusion
  841.7 15.6 %copy.43 = bf16[4,3072,128]{2,0,1:T(4,128)(2,1)} copy(bf16[4,3072,128]{2,1,0:T(8,128)(2,1)S(1)} %add_convert_fusion) | data formatting | bytes 6291456 | tf_op jit(solution)/shard_map/convert_element_type | solution.py:47
  858.2 6.0 all-to-all-start.4
  866.3 67.7 %all-to-all-done.4 = bf16[4,3072,128]{2,0,1:T(4,128)(2,1)S(1)} async-done(((bf16[4,3072,128]{2,0,1:T(4,128)(2,1)}), bf16[4,3072,128]{2,0,1:T(4,128)(2,1)S(1)}, u32[]{:S(2)}, u32[]{:S(2)}) %all-to-all-start.4) | async-done | bytes 3145760 | tf_op jit(solution)/shard_map/all_to_all | solution.py:85
  (182 shorter events, 136.3 us)
Async XLA Ops:
  0.6 117.7 %copy-start.2 = (bf16[4,16,3,192,128]{4,3,2,1,0:T(8,128)(2,1)S(1)}, bf16[4,16,3,192,128]{4,3,2,1,0:T(8,128)(2,1)}, u32[]{:S(2)}) copy-start(bf16[4,16,3,192,128]{4,3,2,1,0:T(8,128)(2,1)} %param.13) | copy-start | bytes 28311556
  327.8 6.6 copy-start.8
  327.8 210.7 %all-to-all-start.1 = ((bf16[64,3,192,128]{3,2,1,0:T(8,128)(2,1)}), bf16[64,3,192,128]{3,2,1,0:T(8,128)(2,1)}, u32[]{:S(2)}, u32[]{:S(2)}) async-start(bf16[64,3,192,128]{3,2,1,0:T(8,128)(2,1)} %bitcast.173), calls=%async_computation.1 | async-start | bytes 18874368 | tf_op jit(solution)/shard_map/all_to_all | solution.py:62
  548.8 280.8 %copy-start.4 = (f32[4,128]{1,0:T(4,128)S(1)}, f32[4,128]{1,0:T(4,128)}, u32[]{:S(2)}) copy-start(f32[4,128]{1,0:T(4,128)} %get-tuple-element.258) | copy-start | bytes 6148
  548.8 280.8 %copy-start.5 = (f32[4,128]{1,0:T(4,128)S(1)}, f32[4,128]{1,0:T(4,128)}, u32[]{:S(2)}) copy-start(f32[4,128]{1,0:T(4,128)} %get-tuple-element.259) | copy-start | bytes 6148
  553.6 3.7 copy-start
  590.8 2.7 copy-start.1
  600.8 2.7 copy-start.1
  610.9 2.7 copy-start.1
  623.8 3.7 copy-start
  661.0 2.7 copy-start.1
  671.0 2.7 copy-start.1
  681.0 2.7 copy-start.1
  694.0 3.7 copy-start
  731.3 2.7 copy-start.1
  741.3 2.7 copy-start.1
  751.3 2.7 copy-start.1
  764.3 3.7 copy-start
  801.4 2.7 copy-start.1
  811.5 2.7 copy-start.1
  821.5 2.7 copy-start.1
  829.6 8.0 copy-start.6
  829.6 8.0 copy-start.7
  832.8 24.5 %all-to-all-start.5 = ((bf16[4,768,128]{2,0,1:T(4,128)(2,1)}), bf16[4,768,128]{2,0,1:T(4,128)(2,1)S(1)}, u32[]{:S(2)}, u32[]{:S(2)}) async-start(bf16[4,768,128]{2,0,1:T(4,128)(2,1)} %copy.45), calls=%async_computation.5 | async-start | bytes 1572864 | tf_op jit(solution)/shard_map/all_to_all | solution.py:88
  857.3 0.9 copy-start.3
  858.2 75.9 %all-to-all-start.4 = ((bf16[4,3072,128]{2,0,1:T(4,128)(2,1)}), bf16[4,3072,128]{2,0,1:T(4,128)(2,1)S(1)}, u32[]{:S(2)}, u32[]{:S(2)}) async-start(bf16[4,3072,128]{2,0,1:T(4,128)(2,1)} %copy.43), calls=%async_computation.4 | async-start | bytes 6291456 | tf_op jit(solution)/shard_map/all_to_all | solution.py:85
where the time goes:
time: 938 us; the launch traced here: 937 us
  blocking collectives  327 us (35%)
  waiting for transfers between devices  253 us (27%)
  matrix products  159 us (17%)
  local copies, waits for them, and re-layouts  98.8 us (11%)
  other arithmetic  79.8 us (9%)
  starting transfers between devices  16.7 us (2%)
    all_to_all x1, blocking collectives, on_device(): lax.all_to_all(to_pairs(video_qkv), 'seq', split_axis=0, concat_axis=2, t...  209 us
    all_to_all x1, waiting for transfers between devices, on_device(): lax.all_to_all(to_pairs(video_cross), 'seq', split_axis=0, concat_axis=2,...  185 us
    dot_general x32, matrix products, one_block(): jnp.dot(shares, values, preferred_element_type=jnp.float32)  108 us
    all_to_all x1, waiting for transfers between devices, on_device(): lax.all_to_all(mix_video, 'seq', split_axis=1, concat_axis=0, tiled=True)  67.7 us
    all_to_all x1, blocking collectives, on_device(): lax.all_to_all(to_pairs(audio_cross), 'seq', split_axis=0, concat_axis=2,...  59.8 us
    all_to_all x1, blocking collectives, on_device(): lax.all_to_all(to_pairs(audio_qkv), 'seq', split_axis=0, concat_axis=2, t...  57.9 us
    reduce_sum x32, other arithmetic, one_block(): row_total = jnp.sum(weights, axis=1, keepdims=True)  51.7 us
    dot_general x32, matrix products, one_block(): lax.dot_general(query_block, key_rows, (((1,), (1,)), ((), ())), preferre...  50.7 us
  transfers between devices with their start and end apart: 3, of which 2 were waited for; matrix products, arithmetic and copies ran while one was open for 4% of the time, Pallas kernels for 0%

commit v1 on v0

v1 whole, which is shorter than its diff:
```python
import functools
import math

import jax
import jax.numpy as jnp
from jax import lax
from jax.experimental import pallas as pl
from jax.experimental.pallas import tpu as pltpu
from jax.sharding import PartitionSpec as P

ROW_TILE = 16
MESH_ID = pl.DeviceIdType.MESH


def attend(queries, key_rows, values, bias, score_scale):
    scores = lax.dot_general(
        queries, key_rows, (((1,), (1,)), ((), ())), preferred_element_type=jnp.float32
    )
    scores = scores * score_scale + bias
    row_max = jnp.max(scores, axis=1, keepdims=True)
    weights = jnp.exp2(scores - row_max)
    row_total = jnp.sum(weights, axis=1, keepdims=True)
    mixed = jnp.dot(weights.astype(jnp.bfloat16), values, preferred_element_type=jnp.float32)
    return (mixed / row_total).astype(jnp.bfloat16).astype(jnp.float32)


def key_bias(total, padded, rows, keep_len):
    column = lax.broadcasted_iota(jnp.int32, (1, total), 1)
    if padded == rows:
        visible = column < keep_len
    else:
        row = column % padded
        visible = (row < rows) & ((column // padded) * rows + row < keep_len)
    return jnp.where(visible, 0.0, -1e30)


def kernel(
    group, clips, heads, local, rows_v, rows_a, pad_a, size,
    vq_hbm, vc_hbm, aq_hbm, ac_hbm, len_ref, gate_ref,
    vout_hbm, aout_hbm,
    vq, vc, aq, ac, vres, ares,
    in_send, in_recv, out_send, out_recv,
):
    me = lax.axis_index("seq")
    total_v, total_a = group * rows_v, group * pad_a
    streams = (
        (vq_hbm, vq, rows_v),
        (aq_hbm, aq, pad_a),
        (vc_hbm, vc, rows_v),
        (ac_hbm, ac, pad_a),
    )

    def clip_head(device, j):
        pair = device * local + j
        return pair // heads, pair % heads

    barrier = pltpu.get_barrier_semaphore()

    def greet(t, carry):
        pl.semaphore_signal(
            barrier, inc=1, device_id={"seq": (me + t) % group}, device_id_type=MESH_ID
        )
        return carry

    lax.fori_loop(1, group, greet, 0)
    pl.semaphore_wait(barrier, group - 1)

    def send_inputs(j):
        def to_one(t, carry):
            there = (me + t) % group
            clip, head = clip_head(there, j)
            for k, (source, buffer, rows) in enumerate(streams):
                pltpu.make_async_remote_copy(
                    src_ref=source.at[clip, head],
                    dst_ref=buffer.at[j, :, pl.ds(pl.multiple_of(me * rows, ROW_TILE), rows), :],
                    send_sem=in_send.at[k, j],
                    recv_sem=in_recv.at[k, j],
                    device_id={"seq": there},
                    device_id_type=MESH_ID,
                ).start()
            return carry

        clip, head = clip_head(me, j)
        for k, (source, buffer, rows) in enumerate(streams):
            pltpu.make_async_copy(
                source.at[clip, head],
                buffer.at[j, :, pl.ds(pl.multiple_of(me * rows, ROW_TILE), rows), :],
                in_recv.at[k, j],
            ).start()
        lax.fori_loop(1, group, to_one, 0)

    results = ((vout_hbm, vres, rows_v), (aout_hbm, ares, pad_a))

    def send_outputs(j, k):
        target, buffer, rows = results[k]
        clip, head = clip_head(me, j)

        def to_one(t, carry):
            there = (me + t) % group
            pltpu.make_async_remote_copy(
                src_ref=buffer.at[j, pl.ds(pl.multiple_of(there * rows, ROW_TILE), rows), :],
                dst_ref=target.at[clip, head],
                send_sem=out_send.at[k, j],
                recv_sem=out_recv.at[k],
                device_id={"seq": there},
                device_id_type=MESH_ID,
            ).start()
            return carry

        pltpu.make_async_copy(
            buffer.at[j, pl.ds(pl.multiple_of(me * rows, ROW_TILE), rows), :],
            target.at[clip, head],
            out_recv.at[k],
        ).start()
        lax.fori_loop(1, group, to_one, 0)

    def wait_bytes(ref, sem):
        pltpu.make_async_copy(ref, ref, sem).wait()

    score_scale = math.log2(math.e) / math.sqrt(size)
    block_v, block_a = math.gcd(total_v, 256), math.gcd(total_a, 256)

    send_inputs(0)
    if local > 1:
        send_inputs(1)

    def one_pair(j, carry):
        for k, (_, buffer, _) in enumerate(streams):
            wait_bytes(buffer.at[j], in_recv.at[k, j])

        @pl.when(j + 2 < local)
        def _():
            send_inputs(j + 2)

        clip, head = clip_head(me, j)
        bias_v = key_bias(total_v, rows_v, rows_v, len_ref[0, clip])
        bias_a = key_bias(total_a, pad_a, rows_a, len_ref[1, clip])
        gates = [gate_ref[k, pl.ds(head, 1), :] for k in range(4)]

        def video_block(i, c):
            rows = pl.ds(pl.multiple_of(i * block_v, block_v), block_v)
            near = attend(vq[j, 0, rows, :], vq[j, 1], vq[j, 2], bias_v, score_scale)
            far = attend(vc[j, 0, rows, :], ac[j, 1], ac[j, 2], bias_a, score_scale)
            vres[j, rows, :] = (gates[0] * near + gates[1] * far).astype(jnp.bfloat16)
            return c

        lax.fori_loop(0, total_v // block_v, video_block, 0)
        send_outputs(j, 0)

        def audio_block(i, c):
            rows = pl.ds(pl.multiple_of(i * block_a, block_a), block_a)
            near = attend(aq[j, 0, rows, :], aq[j, 1], aq[j, 2], bias_a, score_scale)
            far = attend(ac[j, 0, rows, :], vc[j, 1], vc[j, 2], bias_v, score_scale)
            ares[j, rows, :] = (gates[2] * near + gates[3] * far).astype(jnp.bfloat16)
            return c

        lax.fori_loop(0, total_a // block_a, audio_block, 0)
        send_outputs(j, 1)
        return carry

    lax.fori_loop(0, local, one_pair, 0)

    def drain(j, carry):
        for k, (_, buffer, rows) in enumerate(streams):
            wait_bytes(buffer.at[j, :, pl.ds(0, (group - 1) * rows), :], in_send.at[k, j])
        for k, (_, buffer, rows) in enumerate(results):
            wait_bytes(buffer.at[j, pl.ds(0, (group - 1) * rows), :], out_send.at[k, j])
        return carry

    lax.fori_loop(0, local, drain, 0)
    for k, (target, _, _) in enumerate(results):
        wait_bytes(target, out_recv.at[k])


def on_device(video_qkv, video_cross, audio_qkv, audio_cross, lengths, timestep, gate_table):
    group = lax.axis_size("seq")
    clips, heads, _, rows_v, size = video_qkv.shape
    rows_a = audio_qkv.shape[3]
    local = clips * heads // group
    pad_a = -(-rows_a // ROW_TILE) * ROW_TILE
    if pad_a != rows_a:
        extra = ((0, 0), (0, 0), (0, 0), (0, pad_a - rows_a), (0, 0))
        audio_qkv, audio_cross = jnp.pad(audio_qkv, extra), jnp.pad(audio_cross, extra)
    gate_rows = lax.dynamic_index_in_dim(gate_table, timestep[0], 0, keepdims=False)
    total_v, total_a = group * rows_v, group * pad_a
    any_spec = pl.BlockSpec(memory_space=pl.ANY)
    dtype = video_qkv.dtype
    video_out, audio_out = pl.pallas_call(
        functools.partial(kernel, group, clips, heads, local, rows_v, rows_a, pad_a, size),
        out_shape=(
            jax.ShapeDtypeStruct((clips, heads, rows_v, size), dtype),
            jax.ShapeDtypeStruct((clips, heads, pad_a, size), dtype),
        ),
        in_specs=[any_spec] * 4
        + [pl.BlockSpec(memory_space=pltpu.SMEM), pl.BlockSpec(memory_space=pltpu.VMEM)],
        out_specs=(any_spec, any_spec),
        scratch_shapes=[
            pltpu.VMEM((local, 3, total_v, size), dtype),
            pltpu.VMEM((local, 3, total_v, size), dtype),
            pltpu.VMEM((local, 3, total_a, size), dtype),
            pltpu.VMEM((local, 3, total_a, size), dtype),
            pltpu.VMEM((local, total_v, size), dtype),
            pltpu.VMEM((local, total_a, size), dtype),
            pltpu.SemaphoreType.DMA((4, local)),
            pltpu.SemaphoreType.DMA((4, local)),
            pltpu.SemaphoreType.DMA((2, local)),
            pltpu.SemaphoreType.DMA((2,)),
        ],
        compiler_params=pltpu.CompilerParams(
            collective_id=0, has_side_effects=True, vmem_limit_bytes=60000 * 1024
        ),
    )(video_qkv, video_cross, audio_qkv, audio_cross, lengths, gate_rows)
    return (video_out, audio_out[:, :, :rows_a])


def solution(mesh):
    in_specs = (
        P("groups", None, None, "seq", None),
        P("groups", None, None, "seq", None),
        P("groups", None, None, "seq", None),
        P("groups", None, None, "seq", None),
        P(None, "groups"),
        P("groups"),
        P(),
    )
    out_specs = (P("groups", None, "seq", None), P("groups", None, "seq", None))
    return jax.shard_map(
        on_device, mesh=mesh, in_specs=in_specs, out_specs=out_specs, check_vma=False
    )
```

time: 938 us -> 615 us (0.66)
  Pallas kernels: 0 us -> 605 us
  blocking collectives: 327 us -> 0 us
  waiting for transfers between devices: 253 us -> 0 us
  matrix products: 159 us -> 0 us
  local copies, waits for them, and re-layouts: 98.8 us -> 6 us
  other arithmetic: 79.8 us -> 0 us
  starting transfers between devices: 16.7 us -> 0 us
    pallas_call x0 -> x1, Pallas kernels: none -> 605 us  [on_device(): pl.pallas_call(functools.partial(kernel, group, clips, heads, local, rows...]
    all_to_all x3 -> x0, blocking collectives: 327 us -> none  [the longest x1 209 us: on_device(): lax.all_to_all(to_pairs(video_qkv), 'seq', split_axis=0, concat_axis=2, t...]
    all_to_all x3 -> x0, waiting for transfers between devices: 253 us -> none  [the longest x1 185 us: on_device(): lax.all_to_all(to_pairs(video_cross), 'seq', split_axis=0, concat_axis=2,...]
    dot_general x64 -> x0, matrix products: 159 us -> none  [the longest x32 108 us: one_block(): jnp.dot(shares, values, preferred_element_type=jnp.float32)]
    reduce_sum x35 -> x0, other arithmetic: 54.2 us -> none  [the longest x32 51.7 us: one_block(): row_total = jnp.sum(weights, axis=1, keepdims=True)]
    all_to_all x6 -> x0, local copies, waits for them, and re-layouts: 30.7 us -> none  [the longest x1 10.3 us: on_device(): lax.all_to_all(to_pairs(video_cross), 'seq', split_axis=0, concat_axis=2,...]
    lt x32 -> x0, other arithmetic: 19.8 us -> none  [attend(): visible = columns[None, :] < keep_len]
    convert_element_type x2 -> x0, local copies, waits for them, and re-layouts: 17.1 us -> none  [mix_pairs(): return mixed_sum.astype(jnp.bfloat16)]
  transfers between devices with their start and end apart: 3 -> 0, of which waited for: 2 -> 0; matrix products, arithmetic and copies ran while one was open for 4% -> 0% of each run, Pallas kernels for 0% -> 0%
where the time goes in v1:
time: 615 us; the launch traced here: 613 us
  Pallas kernels  605 us (98%)
    pallas_call x1, Pallas kernels, on_device(): pl.pallas_call(functools.partial(kernel, group, clips, heads, local, rows...  605 us

profile of v1, /device:TPU:13, one launch (start us, length us, event | category | flops | bytes accessed | tf_op | source)
XLA Modules:
  0.0 612.7 jit_solution(13473481554665195885)
XLA Ops:
  0.6 0.0 copy-start
  1.4 0.7 copy-done
  2.1 0.6 dynamic-slice_bitcast_fusion.gate_ref
  2.7 605.3 %shard_map.86 = (bf16[4,16,192,128]{3,2,1,0:T(8,128)(2,1)}, bf16[4,16,48,128]{3,2,1,0:T(8,128)(2,1)}) custom-call(bf16[4,16,3,192,128]{4,3,2,1,0:T(8,128)(2,1)} %vq_hbm.1, bf16[4,16,3,192,128]{4,3,2,1,0:T(8,128)(2,1)} %vc_hbm.1, bf16[4,16,3,48,128]{4,3,2,1,0:T(8,128)(2,1)} %aq_hbm.1, bf16[4,16,3,48,128]{4,3,2,1,0:T(8,128)(2,1)} %ac_hbm.1, s32[2,4]{1,0:T(2,128)} %len_ref.1, ...), custom_call_target="tpu_custom_call" | custom-call | tf_op jit(solution)/shard_map/pallas_call | solution.py:188
  608.0 0.0 copy-start.1
  608.0 3.8 copy.12
  611.9 0.0 copy-done.1
  611.9 0.9 copy.13
Async XLA Ops:
  0.6 1.5 copy-start
  608.0 3.8 copy-start.1
